TPU v7x, 512 devices: a whole 4x8x8 slice. The times are simulated.
512 devices in a mesh: row: 16 (over y, core), col: 32 (over z, x).
Axes of the slice: x: 4, y: 8, z: 8, core: 2. Of those that a mesh axis runs over, the one named last changes fastest.
Arguments:
- matrix: float32 [16384, 16384], P('row', 'col'), as said below
Outputs:
- hess_panel: float32 [16384, 8], P('row')
- reflectors: float32 [16384, 8], P('row')
- wy_products: float32 [16384, 8], P('row')
- wy_factor: float32 [8, 8], replicated
Inputs may be any that keep to these rules, and one draw needn't show every extreme that they name: Entries matrix[i+1, i] lie within 2.5 +- 6 / sqrt(16384); every other entry within +- 6 / sqrt(16384).
All inputs are finite; a program needn't handle non-finite values.
Results may differ from a plain program's by a relative error of at most 0.0003.
Values sent between devices are 32-bit elements; how exact they have to be, the bound alone decides.
A program may use at most 128 MiB of HBM per device.

v0:
```python
import jax
import jax.numpy as jnp
from jax import lax
from jax.sharding import PartitionSpec as P

NB = 8


def picked(value, axis, root):
    return lax.dynamic_index_in_dim(lax.all_gather(value, axis), root, 0, keepdims=False)


def copy_for_each(value, axis):
    count = lax.axis_size(axis)
    return lax.all_to_all(
        jnp.broadcast_to(value[None], (count, *value.shape)), axis, 0, 0, tiled=True
    )


def over_copies(value, axis):
    return copy_for_each(value, axis).sum(axis=0)


def packed_total(arrays, axis):
    ravelled, at, outs = (jnp.concatenate([a.reshape(-1) for a in arrays]), 0, [])
    so_far = over_copies(ravelled, axis)
    for a in arrays:
        outs.append(so_far[at : at + a.size].reshape(a.shape))
        at += a.size
    return tuple(outs)


def in_order(tiles, dim):
    shape = list(tiles.shape[1:])
    shape[dim] *= tiles.shape[0]
    return jnp.moveaxis(tiles, 0, dim).reshape(shape)


def collect(value, axis, dim):
    tiles = copy_for_each(value, axis)
    return in_order(tiles, dim)


def shards(matrix):
    exact = lax.Precision.HIGHEST
    rows_local, cols_local = matrix.shape
    row_ids = lax.axis_index("row") * rows_local + lax.iota(jnp.int32, rows_local)
    panel = picked(matrix[:, :NB], "col", 0)
    top_ids = lax.iota(jnp.int32, NB + 1)
    picker = (row_ids[None, :] == top_ids[:, None]).astype(jnp.float32)
    refl = jnp.zeros((rows_local, NB), jnp.float32)
    wy_prod = jnp.zeros((rows_local, NB), jnp.float32)
    factor = jnp.zeros((NB, NB), jnp.float32)
    refl_top = jnp.zeros((NB + 1, NB), jnp.float32)
    gram = jnp.zeros((NB, NB), jnp.float32)
    columns = []
    for column in range(NB):
        current = panel[:, column] - jnp.dot(wy_prod, refl_top[column], precision=exact)
        inner, head_rows, square = packed_total(
            (
                jnp.dot(current, refl, precision=exact),
                jnp.dot(picker, current, precision=exact),
                jnp.sum(current * current),
            ),
            "row",
        )
        weight = jnp.dot(inner, factor, precision=exact)
        upper = refl_top[: column + 1]
        head = head_rows[: column + 1]
        masked_gram = gram - jnp.dot(upper.T, upper, precision=exact)
        masked_inner = inner - jnp.dot(head, upper, precision=exact)
        sumsq = (
            square
            - jnp.sum(head * head)
            - 2.0 * jnp.dot(weight, masked_inner, precision=exact)
            + jnp.dot(weight, jnp.dot(masked_gram, weight, precision=exact), precision=exact)
        )
        leading = head_rows[column + 1] - jnp.dot(refl_top[column + 1], weight, precision=exact)
        current = current - jnp.dot(refl, weight, precision=exact)
        masked = jnp.where(row_ids > column, current, jnp.float32(0.0))
        length = jnp.sqrt(sumsq)
        orient = jnp.where(leading >= 0, jnp.float32(1.0), jnp.float32(-1.0))
        pivot_value = -orient * length
        vector = masked + jnp.where(row_ids == column + 1, orient * length, jnp.float32(0.0))
        vector = vector / jnp.sqrt(length * (length + jnp.abs(leading)))
        whole = collect(vector, "row", 0)
        piece = lax.dynamic_slice_in_dim(whole, lax.axis_index("col") * cols_local, cols_local, 0)
        vec_top = whole[: NB + 1]
        if column > 0:
            coupling = over_copies(jnp.dot(vector, refl, precision=exact), "row")
        else:
            coupling = jnp.zeros((NB,), jnp.float32)
        image = over_copies(jnp.dot(matrix, piece, precision=exact), "col")
        new_y = image - jnp.dot(wy_prod, coupling, precision=exact)
        new_t = -jnp.dot(factor, coupling, precision=exact)
        factor = factor.at[:, column].set(new_t).at[column, column].set(jnp.float32(1.0))
        gram = (
            gram.at[:, column]
            .set(coupling)
            .at[column, :]
            .set(coupling)
            .at[column, column]
            .set(jnp.float32(2.0))
        )
        wy_prod = wy_prod.at[:, column].set(new_y)
        refl = refl.at[:, column].set(vector)
        refl_top = refl_top.at[:, column].set(vec_top)
        columns.append(
            jnp.where(
                row_ids <= column,
                current,
                jnp.where(row_ids == column + 1, pivot_value, jnp.float32(0.0)),
            )
        )
    return (jnp.stack(columns, axis=1), refl, wy_prod, factor)


def solution(mesh):
    return jax.shard_map(
        shards,
        mesh=mesh,
        in_specs=(P("row", "col"),),
        out_specs=(P("row", None), P("row", None), P("row", None), P()),
        check_vma=False,
    )
```

profile of v0, /device:TPU:1, one launch (start us, length us, event | category | flops | bytes accessed | tf_op | source)
XLA Modules:
  0.0 684.6 jit_solution(8023742177994909650)
XLA Ops:
  9.8 152.0 %all-gather.3.cloned.1.call-done = f32[32768,8]{1,0:T(8,128)} async-done(((f32[1024,8]{1,0:T(8,128)}), f32[32768,8]{1,0:T(8,128)}) %all-gather.3.cloned.1.call-update) | async-done | bytes 1048592 | tf_op jit(solution)/shard_map/all_gather | solution.py:10
  169.6 8.1 %all-to-all-start = ((f32[16,1,18]{2,1,0:T(1,128)}), f32[16,1,18]{2,1,0:T(1,128)S(1)}, u32[]{:S(2)}, u32[]{:S(2)}) async-start(f32[16,1,18]{2,1,0:T(1,128)} %broadcast_in_dim.266), calls=%async_computation | async-start | bytes 16384 | tf_op jit(solution)/shard_map/all_to_all | solution.py:15
  178.4 6.3 all-to-all-done
  198.7 7.8 %all-to-all-done.1 = f32[16,1,1024]{2,1,0:T(1,128)S(1)} async-done(((f32[16,1,1024]{2,1,0:T(1,128)}), f32[16,1,1024]{2,1,0:T(1,128)S(1)}, u32[]{:S(2)}, u32[]{:S(2)}) %all-to-all-start.1) | async-done | bytes 65568 | tf_op jit(solution)/shard_map/all_to_all | solution.py:15
  216.8 7.3 %all-to-all-done.2 = f32[32,1,1024]{2,1,0:T(1,128)S(1)} async-done(((f32[32,1,1024]{2,1,0:T(1,128)}), f32[32,1,1024]{2,1,0:T(1,128)S(1)}, u32[]{:S(2)}, u32[]{:S(2)}) %all-to-all-start.2) | async-done | bytes 131104 | tf_op jit(solution)/shard_map/all_to_all | solution.py:15
  232.3 6.9 %all-to-all-done.3 = f32[16,1,18]{2,1,0:T(1,128)S(1)} async-done(((f32[16,1,18]{2,1,0:T(1,128)}), f32[16,1,18]{2,1,0:T(1,128)S(1)}, u32[]{:S(2)}, u32[]{:S(2)}) %all-to-all-start.3) | async-done | bytes 1184 | tf_op jit(solution)/shard_map/all_to_all | solution.py:15
  266.4 5.5 all-to-all-done.4
  279.2 9.0 %all-to-all-done.5 = f32[32,1,1024]{2,1,0:T(1,128)S(1)} async-done(((f32[32,1,1024]{2,1,0:T(1,128)}), f32[32,1,1024]{2,1,0:T(1,128)S(1)}, u32[]{:S(2)}, u32[]{:S(2)}) %all-to-all-start.5) | async-done | bytes 131104 | tf_op jit(solution)/shard_map/all_to_all | solution.py:15
  296.5 6.9 %all-to-all-done.7 = f32[16,1,18]{2,1,0:T(1,128)S(1)} async-done(((f32[16,1,18]{2,1,0:T(1,128)}), f32[16,1,18]{2,1,0:T(1,128)S(1)}, u32[]{:S(2)}, u32[]{:S(2)}) %all-to-all-start.7) | async-done | bytes 1184 | tf_op jit(solution)/shard_map/all_to_all | solution.py:15
  316.6 6.3 all-to-all-done.10
  329.4 5.9 all-to-all-done.8
  342.7 9.0 %all-to-all-done.9 = f32[32,1,1024]{2,1,0:T(1,128)S(1)} async-done(((f32[32,1,1024]{2,1,0:T(1,128)}), f32[32,1,1024]{2,1,0:T(1,128)S(1)}, u32[]{:S(2)}, u32[]{:S(2)}) %all-to-all-start.9) | async-done | bytes 131104 | tf_op jit(solution)/shard_map/all_to_all | solution.py:15
  360.0 6.9 %all-to-all-done.11 = f32[16,1,18]{2,1,0:T(1,128)S(1)} async-done(((f32[16,1,18]{2,1,0:T(1,128)}), f32[16,1,18]{2,1,0:T(1,128)S(1)}, u32[]{:S(2)}, u32[]{:S(2)}) %all-to-all-start.11) | async-done | bytes 1184 | tf_op jit(solution)/shard_map/all_to_all | solution.py:15
  380.1 6.2 all-to-all-done.14
  393.3 5.5 all-to-all-done.12
  406.1 9.0 %all-to-all-done.13 = f32[32,1,1024]{2,1,0:T(1,128)S(1)} async-done(((f32[32,1,1024]{2,1,0:T(1,128)}), f32[32,1,1024]{2,1,0:T(1,128)S(1)}, u32[]{:S(2)}, u32[]{:S(2)}) %all-to-all-start.13) | async-done | bytes 131104 | tf_op jit(solution)/shard_map/all_to_all | solution.py:15
  423.4 6.9 %all-to-all-done.15 = f32[16,1,18]{2,1,0:T(1,128)S(1)} async-done(((f32[16,1,18]{2,1,0:T(1,128)}), f32[16,1,18]{2,1,0:T(1,128)S(1)}, u32[]{:S(2)}, u32[]{:S(2)}) %all-to-all-start.15) | async-done | bytes 1184 | tf_op jit(solution)/shard_map/all_to_all | solution.py:15
  443.5 6.3 all-to-all-done.18
  456.7 5.5 all-to-all-done.16
  469.6 9.0 %all-to-all-done.17 = f32[32,1,1024]{2,1,0:T(1,128)S(1)} async-done(((f32[32,1,1024]{2,1,0:T(1,128)}), f32[32,1,1024]{2,1,0:T(1,128)S(1)}, u32[]{:S(2)}, u32[]{:S(2)}) %all-to-all-start.17) | async-done | bytes 131104 | tf_op jit(solution)/shard_map/all_to_all | solution.py:15
  481.9 14.0 %all-to-all-start.19 = ((f32[16,1,18]{2,1,0:T(1,128)}), f32[16,1,18]{2,1,0:T(1,128)S(1)}, u32[]{:S(2)}, u32[]{:S(2)}) async-start(f32[16,1,18]{2,1,0:T(1,128)} %broadcast_in_dim.296), calls=%async_computation.19 | async-start | bytes 16384 | tf_op jit(solution)/shard_map/all_to_all | solution.py:15
  496.0 6.9 %all-to-all-done.19 = f32[16,1,18]{2,1,0:T(1,128)S(1)} async-done(((f32[16,1,18]{2,1,0:T(1,128)}), f32[16,1,18]{2,1,0:T(1,128)S(1)}, u32[]{:S(2)}, u32[]{:S(2)}) %all-to-all-start.19) | async-done | bytes 1184 | tf_op jit(solution)/shard_map/all_to_all | solution.py:15
  516.2 6.2 all-to-all-done.22
  542.2 9.0 %all-to-all-done.21 = f32[32,1,1024]{2,1,0:T(1,128)S(1)} async-done(((f32[32,1,1024]{2,1,0:T(1,128)}), f32[32,1,1024]{2,1,0:T(1,128)S(1)}, u32[]{:S(2)}, u32[]{:S(2)}) %all-to-all-start.21) | async-done | bytes 131104 | tf_op jit(solution)/shard_map/all_to_all | solution.py:15
  559.5 6.9 %all-to-all-done.23 = f32[16,1,18]{2,1,0:T(1,128)S(1)} async-done(((f32[16,1,18]{2,1,0:T(1,128)}), f32[16,1,18]{2,1,0:T(1,128)S(1)}, u32[]{:S(2)}, u32[]{:S(2)}) %all-to-all-start.23) | async-done | bytes 1184 | tf_op jit(solution)/shard_map/all_to_all | solution.py:15
  579.6 6.3 all-to-all-done.26
  592.7 5.6 all-to-all-done.24
  605.6 9.1 %all-to-all-done.25 = f32[32,1,1024]{2,1,0:T(1,128)S(1)} async-done(((f32[32,1,1024]{2,1,0:T(1,128)}), f32[32,1,1024]{2,1,0:T(1,128)S(1)}, u32[]{:S(2)}, u32[]{:S(2)}) %all-to-all-start.25) | async-done | bytes 131104 | tf_op jit(solution)/shard_map/all_to_all | solution.py:15
  622.9 6.9 %all-to-all-done.27 = f32[16,1,18]{2,1,0:T(1,128)S(1)} async-done(((f32[16,1,18]{2,1,0:T(1,128)}), f32[16,1,18]{2,1,0:T(1,128)S(1)}, u32[]{:S(2)}, u32[]{:S(2)}) %all-to-all-start.27) | async-done | bytes 1184 | tf_op jit(solution)/shard_map/all_to_all | solution.py:15
  637.7 10.1 %all_to_all.186 = f32[16,1,8]{2,1,0:T(1,128)S(1)} all-to-all(f32[16,1,8]{2,1,0:T(1,128)S(1)} %broadcast_in_dim.313), channel_id=1, replica_groups=mesh['row'=16,'col'=32] {'row'}, dimensions={0} | all-to-all | bytes 1024 | tf_op jit(solution)/shard_map/all_to_all | solution.py:15
  653.3 7.0 %all-to-all-done.28 = f32[16,1,1024]{2,1,0:T(1,128)S(1)} async-done(((f32[16,1,1024]{2,1,0:T(1,128)}), f32[16,1,1024]{2,1,0:T(1,128)S(1)}, u32[]{:S(2)}, u32[]{:S(2)}) %all-to-all-start.28) | async-done | bytes 65568 | tf_op jit(solution)/shard_map/all_to_all | solution.py:15
  667.4 9.3 %all-to-all-done.29 = f32[32,1,1024]{2,1,0:T(1,128)S(1)} async-done(((f32[32,1,1024]{2,1,0:T(1,128)}), f32[32,1,1024]{2,1,0:T(1,128)S(1)}, u32[]{:S(2)}, u32[]{:S(2)}) %all-to-all-start.29) | async-done | bytes 131104 | tf_op jit(solution)/shard_map/all_to_all | solution.py:15
  (363 shorter events, 252.6 us)
Async XLA Ops:
  7.2 154.6 %all-gather.3.cloned.1.call-start = ((), (), s32[]{:S(2)}) async-start(), calls=%async_computation.31 | async-start | bytes 17301504 | tf_op jit(solution)/shard_map/all_gather | solution.py:10
  9.8 196.9 %copy-start = (f32[1024,512]{1,0:T(8,128)S(1)}, f32[1024,512]{1,0:T(8,128)}, u32[]{:S(2)}) copy-start(f32[1024,512]{1,0:T(8,128)} %param.121) | copy-start | bytes 6291460
  169.6 15.1 %all-to-all-start = ((f32[16,1,18]{2,1,0:T(1,128)}), f32[16,1,18]{2,1,0:T(1,128)S(1)}, u32[]{:S(2)}, u32[]{:S(2)}) async-start(f32[16,1,18]{2,1,0:T(1,128)} %broadcast_in_dim.266), calls=%async_computation | async-start | bytes 16384 | tf_op jit(solution)/shard_map/all_to_all | solution.py:15
  194.8 11.8 %all-to-all-start.1 = ((f32[16,1,1024]{2,1,0:T(1,128)}), f32[16,1,1024]{2,1,0:T(1,128)S(1)}, u32[]{:S(2)}, u32[]{:S(2)}) async-start(f32[16,1,1024]{2,1,0:T(1,128)} %broadcast_in_dim.270), calls=%async_computation.1 | async-start | bytes 131072 | tf_op jit(solution)/shard_map/all_to_all | solution.py:15
  209.2 14.9 %all-to-all-start.2 = ((f32[32,1,1024]{2,1,0:T(1,128)}), f32[32,1,1024]{2,1,0:T(1,128)S(1)}, u32[]{:S(2)}, u32[]{:S(2)}) async-start(f32[32,1,1024]{2,1,0:T(1,128)} %broadcast_in_dim.271), calls=%async_computation.2 | async-start | bytes 262144 | tf_op jit(solution)/shard_map/all_to_all | solution.py:15
  227.3 11.9 %all-to-all-start.3 = ((f32[16,1,18]{2,1,0:T(1,128)}), f32[16,1,18]{2,1,0:T(1,128)S(1)}, u32[]{:S(2)}, u32[]{:S(2)}) async-start(f32[16,1,18]{2,1,0:T(1,128)} %broadcast_in_dim.272), calls=%async_computation.3 | async-start | bytes 16384 | tf_op jit(solution)/shard_map/all_to_all | solution.py:15
  248.5 10.9 %all-to-all-start.6 = ((f32[16,1,8]{2,1,0:T(1,128)}), f32[16,1,8]{2,1,0:T(1,128)S(1)}, u32[]{:S(2)}, u32[]{:S(2)}) async-start(f32[16,1,8]{2,1,0:T(1,128)} %broadcast_in_dim.277), calls=%async_computation.6 | async-start | bytes 16384 | tf_op jit(solution)/shard_map/all_to_all | solution.py:15
  260.1 11.8 %all-to-all-start.4 = ((f32[16,1,1024]{2,1,0:T(1,128)}), f32[16,1,1024]{2,1,0:T(1,128)S(1)}, u32[]{:S(2)}, u32[]{:S(2)}) async-start(f32[16,1,1024]{2,1,0:T(1,128)} %broadcast_in_dim.275), calls=%async_computation.4 | async-start | bytes 131072 | tf_op jit(solution)/shard_map/all_to_all | solution.py:15
  274.5 13.8 %all-to-all-start.5 = ((f32[32,1,1024]{2,1,0:T(1,128)}), f32[32,1,1024]{2,1,0:T(1,128)S(1)}, u32[]{:S(2)}, u32[]{:S(2)}) async-start(f32[32,1,1024]{2,1,0:T(1,128)} %broadcast_in_dim.276), calls=%async_computation.5 | async-start | bytes 262144 | tf_op jit(solution)/shard_map/all_to_all | solution.py:15
  291.6 11.9 %all-to-all-start.7 = ((f32[16,1,18]{2,1,0:T(1,128)}), f32[16,1,18]{2,1,0:T(1,128)S(1)}, u32[]{:S(2)}, u32[]{:S(2)}) async-start(f32[16,1,18]{2,1,0:T(1,128)} %broadcast_in_dim.278), calls=%async_computation.7 | async-start | bytes 16384 | tf_op jit(solution)/shard_map/all_to_all | solution.py:15
  311.9 10.9 %all-to-all-start.10 = ((f32[16,1,8]{2,1,0:T(1,128)}), f32[16,1,8]{2,1,0:T(1,128)S(1)}, u32[]{:S(2)}, u32[]{:S(2)}) async-start(f32[16,1,8]{2,1,0:T(1,128)} %broadcast_in_dim.283), calls=%async_computation.10 | async-start | bytes 16384 | tf_op jit(solution)/shard_map/all_to_all | solution.py:15
  323.5 11.8 %all-to-all-start.8 = ((f32[16,1,1024]{2,1,0:T(1,128)}), f32[16,1,1024]{2,1,0:T(1,128)S(1)}, u32[]{:S(2)}, u32[]{:S(2)}) async-start(f32[16,1,1024]{2,1,0:T(1,128)} %broadcast_in_dim.281), calls=%async_computation.8 | async-start | bytes 131072 | tf_op jit(solution)/shard_map/all_to_all | solution.py:15
  337.9 13.8 %all-to-all-start.9 = ((f32[32,1,1024]{2,1,0:T(1,128)}), f32[32,1,1024]{2,1,0:T(1,128)S(1)}, u32[]{:S(2)}, u32[]{:S(2)}) async-start(f32[32,1,1024]{2,1,0:T(1,128)} %broadcast_in_dim.282), calls=%async_computation.9 | async-start | bytes 262144 | tf_op jit(solution)/shard_map/all_to_all | solution.py:15
  355.0 11.9 %all-to-all-start.11 = ((f32[16,1,18]{2,1,0:T(1,128)}), f32[16,1,18]{2,1,0:T(1,128)S(1)}, u32[]{:S(2)}, u32[]{:S(2)}) async-start(f32[16,1,18]{2,1,0:T(1,128)} %broadcast_in_dim.284), calls=%async_computation.11 | async-start | bytes 16384 | tf_op jit(solution)/shard_map/all_to_all | solution.py:15
  375.4 10.9 %all-to-all-start.14 = ((f32[16,1,8]{2,1,0:T(1,128)}), f32[16,1,8]{2,1,0:T(1,128)S(1)}, u32[]{:S(2)}, u32[]{:S(2)}) async-start(f32[16,1,8]{2,1,0:T(1,128)} %broadcast_in_dim.289), calls=%async_computation.14 | async-start | bytes 16384 | tf_op jit(solution)/shard_map/all_to_all | solution.py:15
  387.0 11.8 %all-to-all-start.12 = ((f32[16,1,1024]{2,1,0:T(1,128)}), f32[16,1,1024]{2,1,0:T(1,128)S(1)}, u32[]{:S(2)}, u32[]{:S(2)}) async-start(f32[16,1,1024]{2,1,0:T(1,128)} %broadcast_in_dim.287), calls=%async_computation.12 | async-start | bytes 131072 | tf_op jit(solution)/shard_map/all_to_all | solution.py:15
  401.4 13.8 %all-to-all-start.13 = ((f32[32,1,1024]{2,1,0:T(1,128)}), f32[32,1,1024]{2,1,0:T(1,128)S(1)}, u32[]{:S(2)}, u32[]{:S(2)}) async-start(f32[32,1,1024]{2,1,0:T(1,128)} %broadcast_in_dim.288), calls=%async_computation.13 | async-start | bytes 262144 | tf_op jit(solution)/shard_map/all_to_all | solution.py:15
  418.4 11.9 %all-to-all-start.15 = ((f32[16,1,18]{2,1,0:T(1,128)}), f32[16,1,18]{2,1,0:T(1,128)S(1)}, u32[]{:S(2)}, u32[]{:S(2)}) async-start(f32[16,1,18]{2,1,0:T(1,128)} %broadcast_in_dim.290), calls=%async_computation.15 | async-start | bytes 16384 | tf_op jit(solution)/shard_map/all_to_all | solution.py:15
  438.8 10.9 %all-to-all-start.18 = ((f32[16,1,8]{2,1,0:T(1,128)}), f32[16,1,8]{2,1,0:T(1,128)S(1)}, u32[]{:S(2)}, u32[]{:S(2)}) async-start(f32[16,1,8]{2,1,0:T(1,128)} %broadcast_in_dim.295), calls=%async_computation.18 | async-start | bytes 16384 | tf_op jit(solution)/shard_map/all_to_all | solution.py:15
  450.4 11.8 %all-to-all-start.16 = ((f32[16,1,1024]{2,1,0:T(1,128)}), f32[16,1,1024]{2,1,0:T(1,128)S(1)}, u32[]{:S(2)}, u32[]{:S(2)}) async-start(f32[16,1,1024]{2,1,0:T(1,128)} %broadcast_in_dim.293), calls=%async_computation.16 | async-start | bytes 131072 | tf_op jit(solution)/shard_map/all_to_all | solution.py:15
  464.8 13.8 %all-to-all-start.17 = ((f32[32,1,1024]{2,1,0:T(1,128)}), f32[32,1,1024]{2,1,0:T(1,128)S(1)}, u32[]{:S(2)}, u32[]{:S(2)}) async-start(f32[32,1,1024]{2,1,0:T(1,128)} %broadcast_in_dim.294), calls=%async_computation.17 | async-start | bytes 262144 | tf_op jit(solution)/shard_map/all_to_all | solution.py:15
  481.9 21.1 %all-to-all-start.19 = ((f32[16,1,18]{2,1,0:T(1,128)}), f32[16,1,18]{2,1,0:T(1,128)S(1)}, u32[]{:S(2)}, u32[]{:S(2)}) async-start(f32[16,1,18]{2,1,0:T(1,128)} %broadcast_in_dim.296), calls=%async_computation.19 | async-start | bytes 16384 | tf_op jit(solution)/shard_map/all_to_all | solution.py:15
  511.5 10.9 %all-to-all-start.22 = ((f32[16,1,8]{2,1,0:T(1,128)}), f32[16,1,8]{2,1,0:T(1,128)S(1)}, u32[]{:S(2)}, u32[]{:S(2)}) async-start(f32[16,1,8]{2,1,0:T(1,128)} %broadcast_in_dim.301), calls=%async_computation.22 | async-start | bytes 16384 | tf_op jit(solution)/shard_map/all_to_all | solution.py:15
  523.1 11.8 %all-to-all-start.20 = ((f32[16,1,1024]{2,1,0:T(1,128)}), f32[16,1,1024]{2,1,0:T(1,128)S(1)}, u32[]{:S(2)}, u32[]{:S(2)}) async-start(f32[16,1,1024]{2,1,0:T(1,128)} %broadcast_in_dim.299), calls=%async_computation.20 | async-start | bytes 131072 | tf_op jit(solution)/shard_map/all_to_all | solution.py:15
  537.4 13.8 %all-to-all-start.21 = ((f32[32,1,1024]{2,1,0:T(1,128)}), f32[32,1,1024]{2,1,0:T(1,128)S(1)}, u32[]{:S(2)}, u32[]{:S(2)}) async-start(f32[32,1,1024]{2,1,0:T(1,128)} %broadcast_in_dim.300), calls=%async_computation.21 | async-start | bytes 262144 | tf_op jit(solution)/shard_map/all_to_all | solution.py:15
  554.6 11.9 %all-to-all-start.23 = ((f32[16,1,18]{2,1,0:T(1,128)}), f32[16,1,18]{2,1,0:T(1,128)S(1)}, u32[]{:S(2)}, u32[]{:S(2)}) async-start(f32[16,1,18]{2,1,0:T(1,128)} %broadcast_in_dim.302), calls=%async_computation.23 | async-start | bytes 16384 | tf_op jit(solution)/shard_map/all_to_all | solution.py:15
  575.0 10.9 %all-to-all-start.26 = ((f32[16,1,8]{2,1,0:T(1,128)}), f32[16,1,8]{2,1,0:T(1,128)S(1)}, u32[]{:S(2)}, u32[]{:S(2)}) async-start(f32[16,1,8]{2,1,0:T(1,128)} %broadcast_in_dim.307), calls=%async_computation.26 | async-start | bytes 16384 | tf_op jit(solution)/shard_map/all_to_all | solution.py:15
  586.5 11.8 %all-to-all-start.24 = ((f32[16,1,1024]{2,1,0:T(1,128)}), f32[16,1,1024]{2,1,0:T(1,128)S(1)}, u32[]{:S(2)}, u32[]{:S(2)}) async-start(f32[16,1,1024]{2,1,0:T(1,128)} %broadcast_in_dim.305), calls=%async_computation.24 | async-start | bytes 131072 | tf_op jit(solution)/shard_map/all_to_all | solution.py:15
  600.9 13.8 %all-to-all-start.25 = ((f32[32,1,1024]{2,1,0:T(1,128)}), f32[32,1,1024]{2,1,0:T(1,128)S(1)}, u32[]{:S(2)}, u32[]{:S(2)}) async-start(f32[32,1,1024]{2,1,0:T(1,128)} %broadcast_in_dim.306), calls=%async_computation.25 | async-start | bytes 262144 | tf_op jit(solution)/shard_map/all_to_all | solution.py:15
  617.9 11.9 %all-to-all-start.27 = ((f32[16,1,18]{2,1,0:T(1,128)}), f32[16,1,18]{2,1,0:T(1,128)S(1)}, u32[]{:S(2)}, u32[]{:S(2)}) async-start(f32[16,1,18]{2,1,0:T(1,128)} %broadcast_in_dim.308), calls=%async_computation.27 | async-start | bytes 16384 | tf_op jit(solution)/shard_map/all_to_all | solution.py:15
  648.5 11.8 %all-to-all-start.28 = ((f32[16,1,1024]{2,1,0:T(1,128)}), f32[16,1,1024]{2,1,0:T(1,128)S(1)}, u32[]{:S(2)}, u32[]{:S(2)}) async-start(f32[16,1,1024]{2,1,0:T(1,128)} %broadcast_in_dim.311), calls=%async_computation.28 | async-start | bytes 131072 | tf_op jit(solution)/shard_map/all_to_all | solution.py:15
  662.9 13.8 %all-to-all-start.29 = ((f32[32,1,1024]{2,1,0:T(1,128)}), f32[32,1,1024]{2,1,0:T(1,128)S(1)}, u32[]{:S(2)}, u32[]{:S(2)}) async-start(f32[32,1,1024]{2,1,0:T(1,128)} %broadcast_in_dim.312), calls=%async_computation.29 | async-start | bytes 262144 | tf_op jit(solution)/shard_map/all_to_all | solution.py:15
  (4 other events, 83.2 us)
Sparse Core Ops, SparseCore 0:
  11.1 150.6 all-gather.2
where the time goes:
time: 691 us; the launch traced here: 685 us
  waiting for transfers between devices  360 us (52%)
  starting transfers between devices  139 us (20%)
  between operations  48.4 us (7%)
  other arithmetic  43.9 us (6%)
  local copies, waits for them, and re-layouts  42 us (6%)
  matrix products  41.4 us (6%)
  blocking collectives  10.1 us (1%)
    all_to_all x30, waiting for transfers between devices, copy_for_each(): lax.all_to_all(jnp.broadcast_to(value[None], (count, *value.shape)), axis...  208 us
    all_gather x1, waiting for transfers between devices, picked(): lax.all_gather(value, axis)  152 us
    all_to_all x30, starting transfers between devices, copy_for_each(): lax.all_to_all(jnp.broadcast_to(value[None], (count, *value.shape)), axis...  139 us
    another operation x39, other arithmetic  25.7 us
    broadcast_in_dim x31, local copies, waits for them, and re-layouts, copy_for_each(): jnp.broadcast_to(value[None], (count, *value.shape))  19.7 us
    dot_general x8, matrix products, shards(): image = over_copies(jnp.dot(matrix, piece, precision=exact), 'col')  14.5 us
  transfers between devices with their start and end apart: 31, of which 31 were waited for; matrix products, arithmetic and copies ran while one was open for 5% of the time, Pallas kernels for 0%

commit v1 on v0

v1 whole, which is shorter than its diff:
```python
import functools

import jax
import jax.numpy as jnp
from jax import lax
from jax.experimental import pallas as pl
from jax.experimental.pallas import tpu as pltpu
from jax.sharding import PartitionSpec as P

NB = 8
TILE = (8, 128)


def across(value, shift):
    return pltpu.roll(value, shift, 0)


def row_sums(tiles, row):
    half = []
    for i in range(4):
        keep = jnp.where(row < 4, tiles[i], tiles[i + 4])
        give = jnp.where(row < 4, tiles[i + 4], tiles[i])
        half.append(keep + across(give, 4))
    quarter = []
    for i in range(2):
        a, b = half[i], half[i + 2]
        quarter.append(jnp.where(row % 4 < 2, a + across(a, 6), b + across(b, 2)))
    a, b = quarter
    return jnp.where(row % 2 < 1, a + across(a, 7), b + across(b, 1))


def tree(values):
    values = list(values)
    while len(values) > 1:
        paired = [values[i] + values[i + 1] for i in range(0, len(values) - 1, 2)]
        if len(values) % 2:
            paired.append(values[-1])
        values = paired
    return values[0]


def inverse_root(value):
    root = lax.rsqrt(value)
    return root * (1.5 - 0.5 * value * root * root)


def kernel(
    R, C, a_ref, hess_ref, v_ref, y_ref, t_ref,
    abuf, at, colt, first, acol_out, acol, xin, xl, zin, zout, vy,
    uhead, qhead, inv_nu, tcols, hcols, signs,
    a_sem, x_sem, z_sem, vy_sem, acol_sem, send_sem,
):
    f32 = jnp.float32
    r, c = lax.axis_index("row"), lax.axis_index("col")
    half = c - 2 * r
    owner = jnp.logical_and(half >= 0, half <= 1)
    seg_row = c // 2
    seg_half = c % 2
    corner = jnp.logical_and(r == 0, c == 0)
    row = lax.broadcasted_iota(jnp.int32, TILE, 0)
    lane = lax.broadcasted_iota(jnp.int32, TILE, 1)
    lane1 = lane[0:1]
    chunks = a_ref.shape[0] // 128
    blocks = a_ref.shape[1] // 128

    def chunk_copy(m):
        rows = pl.ds(pl.multiple_of(m * 128, 128), 128)
        return pltpu.make_async_copy(a_ref.at[rows, :], abuf.at[rows, :], a_sem.at[m])

    for m in range(chunks):
        chunk_copy(m).start()

    barrier = pltpu.get_barrier_semaphore()

    def greet(to_row, to_col):
        pl.semaphore_signal(
            barrier, inc=1, device_id={"row": to_row, "col": to_col},
            device_id_type=pl.DeviceIdType.MESH,
        )

    @pl.when(jnp.logical_not(corner))
    def _():
        greet(seg_row, 0)

    @pl.when(jnp.logical_not(owner))
    def _():
        greet(seg_row, c)

    for h in range(2):
        @pl.when(half != h)
        def _():
            greet(r, 2 * r + h)

    @pl.when(owner)
    def _():
        def body(k, carry):
            greet(r, (c + 1 + k) % C)
            return carry
        lax.fori_loop(0, C - 1, body, 0)

    zero = jnp.zeros(TILE, f32)
    for i in range(NB + 1):
        xl[i] = zero
    for ref in (uhead, qhead, inv_nu, tcols, hcols):
        ref[...] = zero
    for i in range(2):
        for k in range(9):
            vy[i, 8 * k : 8 * k + 8, :] = zero
    signs[...] = jnp.where(lane == 0, f32(1.0), f32(0.0))

    def turn(m, carry):
        chunk_copy(m).wait()
        rows = pl.ds(pl.multiple_of(m * 128, 128), 128)
        for t in range(blocks):
            at[128 * t : 128 * t + 128, rows] = abuf[rows, 128 * t : 128 * t + 128].T
        return carry

    lax.fori_loop(0, chunks, turn, 0)

    @pl.when(c == 0)
    def _():
        for k in range(NB + 1):
            for m in range(chunks):
                colt[k, m : m + 1, :] = at[k : k + 1, 128 * m : 128 * m + 128]
        unit = jnp.where(jnp.logical_and(row == 4, lane == 0), f32(1.0), f32(0.0))
        lead = colt[0]
        first[0] = jnp.where(row < 4, lead, jnp.where(r == 0, unit, zero))
        first[1] = jnp.where(row < 4, across(lead, 4), zero)
        for k in range(NB):
            acol_out[0, k] = across(colt[k + 1], 4)
            acol_out[1, k] = colt[k + 1]

    expected = (
        jnp.where(c == 0, 2 * R, 0) - jnp.where(corner, 1, 0)
        + jnp.where(owner, R + C - 3, 0) + 2
    )
    pl.semaphore_wait(barrier, expected)

    def remote(src, dst, sent, landed, to_row, to_col):
        return pltpu.make_async_remote_copy(
            src_ref=src, dst_ref=dst, send_sem=sent, recv_sem=landed,
            device_id={"row": to_row, "col": to_col},
            device_id_type=pl.DeviceIdType.MESH,
        )

    def await_bytes(ref, sem):
        pltpu.make_async_copy(ref, ref, sem).wait()

    @pl.when(c == 0)
    def _():
        for h in range(2):
            def body(k, carry):
                to = (r + R // 2 + k) % R

                @pl.when(jnp.logical_or(to != r, 2 * r + h != 0))
                def _():
                    remote(
                        first.at[h], xin.at[0], send_sem.at[0], x_sem.at[0], to, 2 * r + h
                    ).start()
                return carry
            lax.fori_loop(0, R, body, 0)
        for h in range(2):
            @pl.when(2 * r + h != 0)
            def _():
                remote(
                    acol_out.at[h], acol, send_sem.at[1], acol_sem, r, 2 * r + h
                ).start()

    @pl.when(corner)
    def _():
        xin[0] = first[0]
        for k in range(NB):
            acol[k] = acol_out[0, k]

    def column(j, carry):
        @pl.when(jnp.logical_not(jnp.where(j == 0, corner, owner)))
        def _():
            await_bytes(xin.at[j], x_sem.at[j])

        x = xin[j]
        xl[j] = x
        swapped = across(x, 4)
        mine = jnp.where(row < 4, f32(0.0), swapped)

        acc = jnp.zeros((8, 128 * chunks), f32)
        for t in range(blocks):
            spread = jnp.broadcast_to(x[t : t + 1, :], (128, 128)).T
            for k in range(16):
                part = spread[8 * k : 8 * k + 8, :]
                at_row = 128 * t + 8 * k
                acc = acc + at[at_row : at_row + 8, :] * jnp.concatenate([part] * chunks, 1)
        z = row_sums([acc[:, 128 * m : 128 * m + 128] for m in range(chunks)], row)

        sums = row_sums([xl[i] * mine for i in range(NB)], row)
        inner = jnp.sum(sums, axis=1, keepdims=True)
        inner = jnp.sum(jnp.where(lane == row, inner, f32(0.0)), axis=0, keepdims=True)
        square = jnp.sum(mine * mine, axis=0, keepdims=True)
        square = jnp.sum(square, axis=1, keepdims=True)
        shares = inner + jnp.where(lane1 == NB, square, f32(0.0))
        b_top = jnp.where(c == 0, x[0:1], f32(0.0))
        q_top = jnp.where(c == 0, x[4:5], f32(0.0))
        extra = jnp.where(row == 4, shares, jnp.where(row == 5, b_top, q_top))
        extra = jnp.where(row == 7, f32(0.0), extra)
        zout[j, 0] = jnp.where(row < 4, z, extra)
        zout[j, 1] = jnp.where(row < 4, across(z, 4), extra)

        for h in range(2):
            @pl.when(half != h)
            def _():
                slot = (c - (2 * r + h) + C) % C - 1
                remote(
                    zout.at[j, h], zin.at[(C - 1) * j + slot],
                    send_sem.at[2], z_sem.at[j], r, 2 * r + h,
                ).start()

        @pl.when(owner)
        def _():
            base = (C - 1) * j
            await_bytes(zin.at[pl.ds(base, C - 1)], z_sem.at[j])
            total = tree([zin[base + k] for k in range(C - 1)] + [zout[j, half]])
            coef = [jnp.broadcast_to(total[4:5, i : i + 1], TILE) for i in range(NB)]
            norm2 = jnp.broadcast_to(total[4:5, NB : NB + 1], TILE)
            norm2 = norm2 - tree([v * v for v in coef])
            inv_norm = inverse_root(norm2)
            fresh = jnp.where(row < 4, total, swapped)
            fresh = fresh - tree([coef[i] * xl[i] for i in range(NB)])
            fresh = fresh * inv_norm
            xin[j + 1] = fresh

            @pl.when(j < NB - 1)
            def _():
                for k in range(R - 1):
                    away = R // 2 + (k // 2 if k % 2 == 0 else -(k + 1) // 2)
                    remote(
                        xin.at[j + 1], xin.at[j + 1], send_sem.at[3], x_sem.at[j + 1],
                        (r + away) % R, c,
                    ).start()

            @pl.when(jnp.logical_and(j == 0, jnp.logical_not(corner)))
            def _():
                await_bytes(acol, acol_sem)

            norm = norm2[0:1] * inv_norm[0:1]
            top_b, top_q = total[5:6], total[6:7]
            qhead[pl.ds(j, 1), :] = top_q
            top = top_b - tree([coef[i][0:1] * qhead[i : i + 1] for i in range(NB)])
            rest = top * inv_norm[0:1]
            solve = []
            for m in range(NB - 1):
                g = -jnp.broadcast_to(rest[:, m + 1 : m + 2], (1, 128)) * inv_nu[m : m + 1]
                rest = rest + g * uhead[m : m + 1]
                solve.append(g)
            pivot = jnp.sum(jnp.where(lane1 == j + 1, rest, f32(0.0)), axis=1, keepdims=True)
            sign_at = jnp.where(lane1 == j, signs[0:1], f32(0.0))
            sign = jnp.broadcast_to(jnp.sum(sign_at, axis=1, keepdims=True), (1, 128))
            pivot = sign * pivot
            orient = jnp.where(pivot >= 0, f32(1.0), f32(-1.0))
            grown = 1.0 + jnp.abs(pivot)
            inv_root = inverse_root(grown)
            inv_pivot = orient * inv_root
            next_sign = -sign * orient
            unit = jnp.where(lane1 == j + 1, f32(1.0), f32(0.0))
            new_head = (sign * rest + orient * unit) * inv_root
            new_head = jnp.where(lane1 > j, new_head, f32(0.0))

            weights = jnp.sum(
                jnp.where(lane == j + 1, uhead[...], f32(0.0)), axis=1, keepdims=True
            )
            weights = jnp.broadcast_to(weights, TILE)
            tcol = jnp.where(lane1 == j, orient * grown * inv_root, f32(0.0))
            for m in range(NB - 1):
                tcol = tcol + jnp.where(lane1 == m, next_sign * solve[m], f32(0.0))
            used = jnp.sum(weights * tcols[...], axis=0, keepdims=True)
            tcols[pl.ds(j, 1), :] = (tcol - used) * inv_pivot

            hcol = jnp.where(lane1 <= j, sign * signs[0:1] * total[4:5], f32(0.0))
            hcol = hcol + jnp.where(lane1 == j + 1, sign * next_sign * norm, f32(0.0))
            hcols[pl.ds(j, 1), :] = hcol

            turned = across(fresh, 4)
            out = jnp.where(row < 4, turned, acol[j] - next_sign * turned)
            for m in range(NB - 1):
                out = out + jnp.where(row < 4, solve[m], -weights[m : m + 1]) * (
                    vy[half, 8 * m : 8 * m + 8, :]
                )
            out = out * jnp.where(row < 4, sign * inv_root, inv_pivot)
            index = 512 * c + 128 * row + lane
            out = out + jnp.where(
                jnp.logical_and(row < 4, index == j + 1), inv_pivot, f32(0.0)
            )
            out = jnp.where(jnp.logical_and(row < 4, index <= j), f32(0.0), out)
            vy[half, pl.ds(pl.multiple_of(8 * j, 8), 8), :] = out

            uhead[pl.ds(j, 1), :] = new_head
            inv_nu[pl.ds(j, 1), :] = jnp.broadcast_to(inv_pivot, (1, 128))
            signs[...] = jnp.where(lane == j + 1, next_sign, signs[...])

            @pl.when(j < NB - 1)
            def _():
                def body(k, carry):
                    part = vy.at[half, pl.ds(pl.multiple_of(8 * j, 8), 8), :]
                    remote(
                        part, part, send_sem.at[4], vy_sem.at[half], r, (c + 1 + k) % C
                    ).start()
                    return carry
                lax.fori_loop(0, C - 1, body, 0)

            @pl.when(j == NB - 1)
            def _():
                vy[half, 64:72, :] = jnp.where(half == 0, tcols[...], hcols[...])

                def body(k, carry):
                    to = (c + C // 2 + k) % C

                    @pl.when(to != c)
                    def _():
                        part = vy.at[half, 56:72, :]
                        remote(
                            part, part, send_sem.at[5], vy_sem.at[half], r, to
                        ).start()
                    return carry
                lax.fori_loop(0, C, body, 0)

        return carry

    lax.fori_loop(0, NB, column, 0)

    for h in range(2):
        @pl.when(half != h)
        def _():
            await_bytes(vy.at[h], vy_sem.at[h])

    for h in range(2):
        for t in range(4):
            at_lane = 128 * (4 * h + t)
            v_ref[:, at_lane : at_lane + 128] = vy[h, pl.ds(t, 8, stride=8), :]
            y_ref[:, at_lane : at_lane + 128] = vy[h, pl.ds(t + 4, 8, stride=8), :]
    hess_ref[...] = jnp.zeros(hess_ref.shape, f32)
    hess_ref[:, 0:128] = jnp.where(r == 0, vy[1, 64:72, :], f32(0.0))
    t_ref[...] = vy[0, 64:72, 0:NB]

    def await_tiles(count, sem):
        await_bytes(zin.at[pl.ds(0, count)], sem)

    @pl.when(c == 0)
    def _():
        @pl.when(corner)
        def _():
            await_tiles(2 * R - 1, send_sem.at[0])
            await_bytes(acol, send_sem.at[1])

        @pl.when(jnp.logical_not(corner))
        def _():
            await_tiles(2 * R, send_sem.at[0])
            await_bytes(acol_out, send_sem.at[1])

    @pl.when(jnp.logical_not(owner))
    def _():
        await_tiles(2 * NB, send_sem.at[2])

    @pl.when(owner)
    def _():
        await_tiles(NB, send_sem.at[2])
        await_tiles((NB - 1) * (R - 1), send_sem.at[3])
        await_tiles((NB - 1) * (C - 1), send_sem.at[4])
        await_tiles(2 * (C - 1), send_sem.at[5])


def shards(R, C, matrix):
    rows, cols = matrix.shape
    f32 = jnp.float32
    wide = jax.ShapeDtypeStruct((NB, rows), f32)
    vmem = pl.BlockSpec(memory_space=pltpu.VMEM)
    scratch = [
        pltpu.VMEM((rows, cols), f32),
        pltpu.VMEM((cols, rows), f32),
        pltpu.VMEM((NB + 1, 8, 128), f32),
        pltpu.VMEM((2, 8, 128), f32),
        pltpu.VMEM((2, NB, 8, 128), f32),
        pltpu.VMEM((NB, 8, 128), f32),
        pltpu.VMEM((NB + 1, 8, 128), f32),
        pltpu.VMEM((NB + 1, 8, 128), f32),
        pltpu.VMEM((NB * (C - 1), 8, 128), f32),
        pltpu.VMEM((NB, 2, 8, 128), f32),
        pltpu.VMEM((2, 72, 128), f32),
    ]
    scratch += [pltpu.VMEM((8, 128), f32)] * 6
    scratch += [
        pltpu.SemaphoreType.DMA((rows // 128,)),
        pltpu.SemaphoreType.DMA((NB,)),
        pltpu.SemaphoreType.DMA((NB,)),
        pltpu.SemaphoreType.DMA((2,)),
        pltpu.SemaphoreType.DMA,
        pltpu.SemaphoreType.DMA((6,)),
    ]
    hess, refl, prod, factor = pl.pallas_call(
        functools.partial(kernel, R, C),
        out_shape=(wide, wide, wide, jax.ShapeDtypeStruct((NB, NB), f32)),
        in_specs=[pl.BlockSpec(memory_space=pl.ANY)],
        out_specs=(vmem,) * 4,
        scratch_shapes=scratch,
        compiler_params=pltpu.CompilerParams(collective_id=0, has_side_effects=True),
        name="panel",
    )(matrix)
    return hess.T, refl.T, prod.T, factor.T


def solution(mesh):
    R, C = mesh.shape["row"], mesh.shape["col"]
    return jax.shard_map(
        functools.partial(shards, R, C),
        mesh=mesh,
        in_specs=(P("row", "col"),),
        out_specs=(P("row", None), P("row", None), P("row", None), P()),
        check_vma=False,
    )
```

time: 691 us -> 112 us (0.16)
  the two profiles are of different devices: /device:TPU:1 before, /device:TPU:33 now
where the time goes in v1:
time: 112 us; the launch traced here: 111 us
  Pallas kernels  105 us (94%)
  local copies, waits for them, and re-layouts  5.46 us (5%)
    pallas_call x1, Pallas kernels, shards(): pl.pallas_call(functools.partial(kernel, R, C), out_shape=(wide, wide, wi...  105 us
    unnamed x4, local copies, waits for them, and re-layouts  5.46 us

profile of v1, /device:TPU:33, one launch (start us, length us, event | category | flops | bytes accessed | tf_op | source)
XLA Modules:
  0.0 111.2 jit_solution(776733777085437125)
XLA Ops:
  0.6 105.1 %panel.1 = (f32[8,1024]{1,0:T(8,128)}, f32[8,1024]{1,0:T(8,128)}, f32[8,1024]{1,0:T(8,128)}, f32[8,8]{1,0:T(8,128)}) custom-call(f32[1024,512]{1,0:T(8,128)} %a_ref.1), custom_call_target="tpu_custom_call" | custom-call | tf_op jit(solution)/shard_map/panel/pallas_call | solution.py:396
  105.7 1.3 %copy.5 = f32[8,8]{1,0:T(8,128)} copy(f32[8,8]{0,1:T(8,128)} %bitcast.7) | data formatting | bytes 512
  107.0 1.4 %copy.9 = f32[1024,8]{0,1:T(8,128)} copy(f32[1024,8]{0,1:T(8,128)} %bitcast.6) | data formatting | bytes 65536
  108.4 1.4 %copy.10 = f32[1024,8]{0,1:T(8,128)} copy(f32[1024,8]{0,1:T(8,128)} %bitcast.5) | data formatting | bytes 65536
  109.8 1.4 %copy.11 = f32[1024,8]{0,1:T(8,128)} copy(f32[1024,8]{0,1:T(8,128)} %bitcast.4) | data formatting | bytes 65536
